TPU v7x, 512 devices: a whole 4x8x8 slice. The times are simulated.
512 devices in a mesh: dp: 32 (over y_hi, x, core), mp: 16 (over y_lo, z).
Axes of the slice: x: 4, y: 8 (y_hi: 4, y_lo: 2; y = y_hi * 2 + y_lo), z: 8, core: 2. Of those that a mesh axis runs over, the one named last changes fastest.
Arguments:
- activations: bfloat16 [32, 128, 4096], P('dp', None, 'mp'), may hold values from -6 to 6
- gradients: bfloat16 [32, 128, 11008], P('dp', None, 'mp'), may hold values from -12 to 12, as said below
- basis_in: bfloat16 [4096, 4096], P(None, 'mp'), may hold values from -0.09375 to 0.09375
- basis_out: bfloat16 [11008, 11008], P('mp', 'dp'), may hold values from -0.0546875 to 0.0546875
Outputs:
- eigen_diag: float32 [11008, 4096], P('dp', 'mp')
Inputs may be any that keep to these rules, and one draw needn't show every extreme that they name: `gradients`: gradients are real-valued with varying scales.
All inputs are finite; a program needn't handle non-finite values.
Results may differ from a plain program's by a relative error of at most 0.02.
Values may be sent and summed in bfloat16 or wider, within the bound.
A program may use at most 64 MiB of HBM per device.

v0:
```python
import jax
import jax.numpy as jnp
from jax import lax
from jax.sharding import PartitionSpec as P


def sent_to_all(shard, axis):
    count = lax.axis_size(axis)
    return lax.all_to_all(
        jnp.broadcast_to(shard[None], (count, *shard.shape)), axis, 0, 0, tiled=True
    )


def joined_along(tiles, dim):
    dims = list(tiles.shape[1:])
    dims[dim] *= tiles.shape[0]
    return jnp.moveaxis(tiles, 0, dim).reshape(dims)


def collect(shard, axis, dim):
    tiles = sent_to_all(shard, axis)
    return joined_along(tiles, dim)


def shards(activations, gradients, basis_in, basis_out):
    gathered = lax.all_gather(gradients, "dp", axis=0, tiled=True)
    seq_count = gathered.shape[0]
    seq_tokens = gathered.shape[1]
    flat_rows = gathered.reshape(seq_count * seq_tokens, gathered.shape[2])
    out_width = basis_out.shape[1]
    partial_sum = jnp.dot(flat_rows, basis_out, preferred_element_type=jnp.float32)
    proj_grad = lax.psum(partial_sum.astype(jnp.bfloat16), "mp")
    proj_grad = proj_grad.reshape(seq_count, seq_tokens, out_width)
    whole_acts = collect(activations, "mp", 2)
    local_tokens = whole_acts.shape[0] * whole_acts.shape[1]
    act_rows = whole_acts.reshape(local_tokens, whole_acts.shape[2])
    proj_act = jnp.dot(act_rows, basis_in, preferred_element_type=jnp.float32).astype(jnp.bfloat16)
    proj_act = proj_act.reshape(whole_acts.shape[0], whole_acts.shape[1], basis_in.shape[1])
    every_act = collect(proj_act, "dp", 0)
    seq_grad = jnp.einsum("sti,stj->sij", proj_grad, every_act, preferred_element_type=jnp.float32)
    squares = jnp.sum(seq_grad * seq_grad, axis=0)
    return squares * (1.0 / (seq_count * seq_tokens))


def solution(mesh):
    return jax.shard_map(
        shards,
        mesh=mesh,
        in_specs=(P("dp", None, "mp"), P("dp", None, "mp"), P(None, "mp"), P("mp", "dp")),
        out_specs=P("dp", "mp"),
        check_vma=False,
    )
```

profile of v0, /device:TPU:2, one launch (start us, length us, event | category | flops | bytes accessed | tf_op | source)
XLA Modules:
  0.0 298.8 jit_solution(9737288411021023752)
XLA Ops:
  6.5 0.0 copy-start
  6.5 0.0 all-gather.2.cloned.1.call-start
  6.5 0.7 all-gather.2.cloned.1.call-update
  7.3 0.9 copy.11
  8.2 0.2 broadcast_in_dim.14
  8.4 37.5 %all_to_all.10 = bf16[16,1,128,256]{2,3,1,0:T(8,128)(2,1)S(1)} all-to-all(bf16[16,1,128,256]{2,3,1,0:T(8,128)(2,1)S(1)} %broadcast_in_dim.14), channel_id=1, replica_groups=mesh['dp'=32,'mp'=16] {'mp'}, dimensions={0} | all-to-all | bytes 2097152 | tf_op jit(solution)/shard_map/all_to_all | solution.py:9
  46.0 0.0 copy-done
  46.0 0.6 convolution_convert_fusion
  46.5 0.0 copy-start.1
  46.6 1.6 broadcast_in_dim.15
  48.2 9.5 %all-to-all-start.1 = ((bf16[32,1,128,256]{3,2,1,0:T(8,128)(2,1)}), bf16[32,1,128,256]{3,2,1,0:T(8,128)(2,1)}, u32[]{:S(2)}, u32[]{:S(2)}) async-start(bf16[32,1,128,256]{3,2,1,0:T(8,128)(2,1)} %broadcast_in_dim.15), calls=%async_computation.1 | async-start | bytes 4194304 | tf_op jit(solution)/shard_map/all_to_all | solution.py:9
  57.7 0.0 all-reduce.2.cloned.1.call-start
  57.8 57.5 %all-gather.2.cloned.1.call-done = bf16[32,128,688]{1,2,0:T(8,128)(2,1)} async-done(((bf16[1,128,688]{1,2,0:T(8,128)(2,1)}), bf16[32,128,688]{1,2,0:T(8,128)(2,1)}) %all-gather.2.cloned.1.call-update) | async-done | bytes 5636112 | tf_op jit(solution)/shard_map/all_gather | solution.py:26
  115.3 0.0 copy-done.1
  115.3 5.0 %fusion.7 = bf16[43,32,8,128]{3,2,1,0:T(8,128)(2,1)S(1)} fusion(bf16[688,344]{1,0:T(8,128)(2,1)S(1)} %copy-done.1, bf16[32,128,688]{1,2,0:T(8,128)(2,1)} %all-gather.2.cloned.1.call-done), kind=kOutput, calls=%fused_computation.7 | convolution fusion | flops 1940226048 | bytes 8927488 | tf_op jit(solution)/shard_map/dot_general | solution.py:31
  120.3 2.1 copy.24
  122.4 0.0 all-reduce.2.cloned.1.call-update
  122.4 9.0 %all-to-all-done.1 = bf16[32,1,128,256]{3,2,1,0:T(8,128)(2,1)} async-done(((bf16[32,1,128,256]{3,2,1,0:T(8,128)(2,1)}), bf16[32,1,128,256]{3,2,1,0:T(8,128)(2,1)}, u32[]{:S(2)}, u32[]{:S(2)}) %all-to-all-start.1) | async-done | bytes 2097184 | tf_op jit(solution)/shard_map/all_to_all | solution.py:9
  131.3 155.8 %all-reduce.2.cloned.1.call-done = bf16[32,128,344]{1,2,0:T(8,128)(2,1)} async-done(((bf16[32,128,344]{1,2,0:T(8,128)(2,1)}), bf16[32,128,344]{1,2,0:T(8,128)(2,1)}) %all-reduce.2.cloned.1.call-update) | async-done | bytes 2818064 | tf_op jit(solution)/shard_map/psum | solution.py:32
  287.1 4.1 %multiply_reduce_fusion = f32[344,256]{1,0:T(8,128)S(1)} fusion(bf16[32,128,344]{1,2,0:T(8,128)(2,1)} %all-reduce.2.cloned.1.call-done, bf16[32,1,128,256]{3,2,1,0:T(8,128)(2,1)} %all-to-all-done.1), kind=kOutput, calls=%fused_computation | convolution fusion | flops 726968320 | bytes 5267456 | tf_op jit(solution)/shard_map/sti,stj->sij/dot_general | solution.py:40
  291.2 0.8 broadcast_multiply_fusion
Async XLA Ops:
  6.5 39.4 %copy-start = (bf16[4096,256]{1,0:T(8,128)(2,1)S(1)}, bf16[4096,256]{1,0:T(8,128)(2,1)}, u32[]{:S(2)}) copy-start(bf16[4096,256]{1,0:T(8,128)(2,1)} %param.6) | copy-start | bytes 6291460
  6.5 108.7 %all-gather.2.cloned.1.call-start = ((), (), s32[]{:S(2)}) async-start(), calls=%async_computation.2 | async-start | bytes 5812224 | tf_op jit(solution)/shard_map/all_gather | solution.py:26
  46.5 68.7 %copy-start.1 = (bf16[688,344]{1,0:T(8,128)(2,1)S(1)}, bf16[688,344]{1,0:T(8,128)(2,1)}, u32[]{:S(2)}) copy-start(bf16[688,344]{1,0:T(8,128)(2,1)} %param.7) | copy-start | bytes 1420036
  48.2 83.1 %all-to-all-start.1 = ((bf16[32,1,128,256]{3,2,1,0:T(8,128)(2,1)}), bf16[32,1,128,256]{3,2,1,0:T(8,128)(2,1)}, u32[]{:S(2)}, u32[]{:S(2)}) async-start(bf16[32,1,128,256]{3,2,1,0:T(8,128)(2,1)} %broadcast_in_dim.15), calls=%async_computation.1 | async-start | bytes 4194304 | tf_op jit(solution)/shard_map/all_to_all | solution.py:9
  57.7 229.4 %all-reduce.2.cloned.1.call-start = ((), (), s32[]{:S(2)}) async-start(), calls=%async_computation.3 | async-start | bytes 5636096 | tf_op jit(solution)/shard_map/psum | solution.py:32
Sparse Core Ops, SparseCore 0:
  10.5 104.6 all-gather.1
  122.5 164.5 all-reduce.1
where the time goes:
time: 299 us
  waiting for transfers between devices  223 us (75%)
  blocking collectives  37.5 us (13%)
  between operations  13.5 us (5%)
  matrix products  9.65 us (3%)
  starting transfers between devices  9.55 us (3%)
  local copies, waits for them, and re-layouts  4.9 us (2%)
    psum x1, waiting for transfers between devices, shards(): proj_grad = lax.psum(partial_sum.astype(jnp.bfloat16), 'mp')  156 us
    all_gather x1, waiting for transfers between devices, shards(): gathered = lax.all_gather(gradients, 'dp', axis=0, tiled=True)  57.5 us
    all_to_all x1, blocking collectives, sent_to_all(): lax.all_to_all(jnp.broadcast_to(shard[None], (count, *shard.shape)), axis...  37.5 us
    all_to_all x1, starting transfers between devices, sent_to_all(): lax.all_to_all(jnp.broadcast_to(shard[None], (count, *shard.shape)), axis...  9.5 us
    all_to_all x1, waiting for transfers between devices, sent_to_all(): lax.all_to_all(jnp.broadcast_to(shard[None], (count, *shard.shape)), axis...  8.96 us
  transfers between devices with their start and end apart: 3, of which 3 were waited for; matrix products, arithmetic and copies ran while one was open for 4% of the time, Pallas kernels for 0%

commit v1 on v0

--- a/solution.py
+++ b/solution.py
@@ -23,7 +23,9 @@
 
 
 def shards(activations, gradients, basis_in, basis_out):
-    gathered = lax.all_gather(gradients, "dp", axis=0, tiled=True)
+    gathered = jnp.concatenate(
+        lax.all_to_all(jnp.stack([gradients] * lax.axis_size("dp")), "dp", 0, 0), axis=0
+    )
     seq_count = gathered.shape[0]
     seq_tokens = gathered.shape[1]
     flat_rows = gathered.reshape(seq_count * seq_tokens, gathered.shape[2])

time: 299 us -> 380 us (1.27)
  waiting for transfers between devices: 223 us -> 285 us
  starting transfers between devices: 9.55 us -> 22.6 us
  local copies, waits for them, and re-layouts: 4.9 us -> 12.4 us
    all_to_all x0 -> x1, waiting for transfers between devices: none -> 120 us  [shards(): lax.all_to_all(jnp.stack([gradients] * lax.axis_size('dp')), 'dp', 0, 0)]
    all_gather x1 -> x0, waiting for transfers between devices: 57.5 us -> none  [shards(): gathered = lax.all_gather(gradients, 'dp', axis=0, tiled=True)]
    all_to_all x1, waiting for transfers between devices: 8.96 us -> 51.3 us  [sent_to_all(): lax.all_to_all(jnp.broadcast_to(shard[None], (count, *shard.shape)), axis...]
    psum x1, waiting for transfers between devices: 156 us -> 114 us  [shards(): proj_grad = lax.psum(partial_sum.astype(jnp.bfloat16), 'mp')]
    all_to_all x0 -> x1, starting transfers between devices: none -> 9.4 us  [shards(): lax.all_to_all(jnp.stack([gradients] * lax.axis_size('dp')), 'dp', 0, 0)]
    all_to_all x0 -> x1, local copies, waits for them, and re-layouts: none -> 4.1 us  [shards(): lax.all_to_all(jnp.stack([gradients] * lax.axis_size('dp')), 'dp', 0, 0)]
  transfers between devices with their start and end apart: 3 -> 3, of which waited for: 3 -> 3; matrix products, arithmetic and copies ran while one was open for 4% -> 3% of each run, Pallas kernels for 0% -> 0%
where the time goes in v1:
time: 380 us; the launch traced here: 379 us
  waiting for transfers between devices  285 us (75%)
  blocking collectives  37.5 us (10%)
  starting transfers between devices  22.6 us (6%)
  between operations  13.5 us (4%)
  local copies, waits for them, and re-layouts  12.4 us (3%)
  matrix products  7.91 us (2%)
    all_to_all x1, waiting for transfers between devices, shards(): lax.all_to_all(jnp.stack([gradients] * lax.axis_size('dp')), 'dp', 0, 0)  120 us
    psum x1, waiting for transfers between devices, shards(): proj_grad = lax.psum(partial_sum.astype(jnp.bfloat16), 'mp')  114 us
    all_to_all x1, waiting for transfers between devices, sent_to_all(): lax.all_to_all(jnp.broadcast_to(shard[None], (count, *shard.shape)), axis...  51.3 us
    all_to_all x1, blocking collectives, sent_to_all(): lax.all_to_all(jnp.broadcast_to(shard[None], (count, *shard.shape)), axis...  37.5 us
    all_to_all x1, starting transfers between devices, sent_to_all(): lax.all_to_all(jnp.broadcast_to(shard[None], (count, *shard.shape)), axis...  13.1 us
    all_to_all x1, starting transfers between devices, shards(): lax.all_to_all(jnp.stack([gradients] * lax.axis_size('dp')), 'dp', 0, 0)  9.4 us
  transfers between devices with their start and end apart: 3, of which 3 were waited for; matrix products, arithmetic and copies ran while one was open for 3% of the time, Pallas kernels for 0%

profile of v1, /device:TPU:2, one launch (start us, length us, event | category | flops | bytes accessed | tf_op | source)
XLA Modules:
  0.0 379.4 jit_solution(6745929031014641979)
XLA Ops:
  6.5 0.0 copy-start
  6.5 0.0 copy-start.1
  6.5 1.1 copy.15
  7.7 0.2 broadcast_in_dim.14
  7.9 37.5 %all_to_all.15 = bf16[16,1,128,256]{2,3,1,0:T(8,128)(2,1)S(1)} all-to-all(bf16[16,1,128,256]{2,3,1,0:T(8,128)(2,1)S(1)} %broadcast_in_dim.14), channel_id=1, replica_groups=mesh['dp'=32,'mp'=16] {'mp'}, dimensions={0} | all-to-all | bytes 2097152 | tf_op jit(solution)/shard_map/all_to_all | solution.py:9
  45.4 0.0 copy-done.1
  45.4 3.2 stack.2
  48.6 9.4 %all-to-all-start = ((bf16[32,1,128,688]{2,3,1,0:T(8,128)(2,1)}), bf16[32,1,128,688]{2,3,1,0:T(8,128)(2,1)}, u32[]{:S(2)}, u32[]{:S(2)}) async-start(bf16[32,1,128,688]{2,3,1,0:T(8,128)(2,1)} %stack.2), calls=%async_computation | async-start | bytes 11272192 | tf_op jit(solution)/shard_map/all_to_all | solution.py:27
  58.0 0.0 copy-done
  58.0 0.6 convolution_convert_fusion
  58.6 119.5 %all-to-all-done = bf16[32,1,128,688]{2,3,1,0:T(8,128)(2,1)} async-done(((bf16[32,1,128,688]{2,3,1,0:T(8,128)(2,1)}), bf16[32,1,128,688]{2,3,1,0:T(8,128)(2,1)}, u32[]{:S(2)}, u32[]{:S(2)}) %all-to-all-start) | async-done | bytes 5636128 | tf_op jit(solution)/shard_map/all_to_all | solution.py:27
  178.2 1.6 broadcast_in_dim.15
  179.8 13.1 %all-to-all-start.2 = ((bf16[32,1,128,256]{3,2,1,0:T(8,128)(2,1)}), bf16[32,1,128,256]{3,2,1,0:T(8,128)(2,1)}, u32[]{:S(2)}, u32[]{:S(2)}) async-start(bf16[32,1,128,256]{3,2,1,0:T(8,128)(2,1)} %broadcast_in_dim.15), calls=%async_computation.2 | async-start | bytes 4194304 | tf_op jit(solution)/shard_map/all_to_all | solution.py:9
  192.9 0.0 copy-start.2
  193.0 0.0 all-reduce.2.cloned.1.call-start
  193.0 4.1 %copy.13 = bf16[32,1,128,688]{2,0,3,1:T(8,128)(2,1)S(1)} copy(bf16[32,1,128,688]{2,3,1,0:T(8,128)(2,1)} %all-to-all-done) | data formatting | bytes 11272192 | tf_op jit(solution)/shard_map/all_to_all | solution.py:27
  197.1 0.0 copy-done.2
  197.1 3.3 fusion.7
  200.4 2.1 copy.28
  202.5 0.0 all-reduce.2.cloned.1.call-update
  202.5 51.3 %all-to-all-done.2 = bf16[32,1,128,256]{3,2,1,0:T(8,128)(2,1)} async-done(((bf16[32,1,128,256]{3,2,1,0:T(8,128)(2,1)}), bf16[32,1,128,256]{3,2,1,0:T(8,128)(2,1)}, u32[]{:S(2)}, u32[]{:S(2)}) %all-to-all-start.2) | async-done | bytes 2097184 | tf_op jit(solution)/shard_map/all_to_all | solution.py:9
  253.8 113.9 %all-reduce.2.cloned.1.call-done = bf16[32,128,344]{1,2,0:T(8,128)(2,1)} async-done(((bf16[32,128,344]{1,2,0:T(8,128)(2,1)}), bf16[32,128,344]{1,2,0:T(8,128)(2,1)}) %all-reduce.2.cloned.1.call-update) | async-done | bytes 2818064 | tf_op jit(solution)/shard_map/psum | solution.py:34
  367.7 4.1 %multiply_reduce_fusion = f32[344,256]{1,0:T(8,128)S(1)} fusion(bf16[32,128,344]{1,2,0:T(8,128)(2,1)} %all-reduce.2.cloned.1.call-done, bf16[32,1,128,256]{3,2,1,0:T(8,128)(2,1)} %all-to-all-done.2), kind=kOutput, calls=%fused_computation | convolution fusion | flops 726968320 | bytes 5267456 | tf_op jit(solution)/shard_map/sti,stj->sij/dot_general | solution.py:42
  371.8 0.8 broadcast_multiply_fusion
Async XLA Ops:
  6.5 51.5 %copy-start = (bf16[4096,256]{1,0:T(8,128)(2,1)S(1)}, bf16[4096,256]{1,0:T(8,128)(2,1)}, u32[]{:S(2)}) copy-start(bf16[4096,256]{1,0:T(8,128)(2,1)} %param.6) | copy-start | bytes 6291460
  6.5 38.9 %copy-start.1 = (bf16[1,128,688]{1,2,0:T(8,128)(2,1)S(1)}, bf16[1,128,688]{1,2,0:T(8,128)(2,1)}, u32[]{:S(2)}) copy-start(bf16[1,128,688]{1,2,0:T(8,128)(2,1)} %param.5) | copy-start | bytes 528388
  48.6 129.5 %all-to-all-start = ((bf16[32,1,128,688]{2,3,1,0:T(8,128)(2,1)}), bf16[32,1,128,688]{2,3,1,0:T(8,128)(2,1)}, u32[]{:S(2)}, u32[]{:S(2)}) async-start(bf16[32,1,128,688]{2,3,1,0:T(8,128)(2,1)} %stack.2), calls=%async_computation | async-start | bytes 11272192 | tf_op jit(solution)/shard_map/all_to_all | solution.py:27
  179.8 74.0 %all-to-all-start.2 = ((bf16[32,1,128,256]{3,2,1,0:T(8,128)(2,1)}), bf16[32,1,128,256]{3,2,1,0:T(8,128)(2,1)}, u32[]{:S(2)}, u32[]{:S(2)}) async-start(bf16[32,1,128,256]{3,2,1,0:T(8,128)(2,1)} %broadcast_in_dim.15), calls=%async_computation.2 | async-start | bytes 4194304 | tf_op jit(solution)/shard_map/all_to_all | solution.py:9
  192.9 4.2 %copy-start.2 = (bf16[688,344]{1,0:T(8,128)(2,1)S(1)}, bf16[688,344]{1,0:T(8,128)(2,1)}, u32[]{:S(2)}) copy-start(bf16[688,344]{1,0:T(8,128)(2,1)} %param.7) | copy-start | bytes 1420036
  193.0 174.8 %all-reduce.2.cloned.1.call-start = ((), (), s32[]{:S(2)}) async-start(), calls=%async_computation.3 | async-start | bytes 5636096 | tf_op jit(solution)/shard_map/psum | solution.py:34
Sparse Core Ops, SparseCore 0:
  202.6 165.0 all-reduce.1
